TPU v7x, 32 devices: a whole 2x2x4 slice. The times are simulated.
32 devices in a mesh: range: 8 (over z, y), depth: 4 (over x, core).
Axes of the slice: x: 2, y: 2, z: 4, core: 2. Of those that a mesh axis runs over, the one named last changes fastest.
Arguments:
- pressure: float32 [4096, 1024], P('depth', 'range'), may hold values from -6 to 6
- vel_range: float32 [4096, 1024], P('depth', 'range'), may hold values from -3 to 3
- vel_depth: float32 [4096, 1024], P('depth', 'range'), may hold values from -3 to 3
- sound_speed: float32 [4096, 1024], P('depth', 'range'), may hold values from 0.5 to 1.1
- density: float32 [4096, 1024], P('depth', 'range'), may hold values from 1 to 3
- ahead_speed: float32 [4096, 64], P('depth'), may hold values from 0.5 to 1.1
- ahead_density: float32 [4096, 64], P('depth'), may hold values from 1 to 3
- shifts: int32 [4], replicated, may hold values from 1 to 16, as said below
- sources: int32 [8, 2], replicated, may hold values from 0 to 4095, as said below
- wavelet: float32 [8, 4], replicated, may hold values from -12 to 12
Outputs:
- pressure_out: float32 [4096, 1024], P('depth', 'range')
- range_out: float32 [4096, 1024], P('depth', 'range')
- depth_out: float32 [4096, 1024], P('depth', 'range')
Inputs may be any that keep to these rules, and one draw needn't show every extreme that they name: `shifts`: every draw has a step that advances by exactly 16 columns. `sources`: column 0 is a depth index below 4096, column 1 a range index below 1024.
All inputs are finite; a program needn't handle non-finite values.
Results may differ from a plain program's by a relative error of at most 0.0003.
Values sent between devices are 32-bit elements; how exact they have to be, the bound alone decides.
No kernel may reach another device: no remote copies, remote signals or barrier semaphores. Data moves between devices by JAX's collectives and lax.ppermute only.
A program may use at most 64 MiB of HBM per device.

v0:
```python
import jax
import jax.numpy as jnp
from jax import lax
from jax.sharding import PartitionSpec as P

ITERS = 4


TIME_STEP = 0.6


def shifted(shard, axis, by):
    size = lax.axis_size(axis)
    pairs = [(i, i + by) for i in range(size) if 0 <= i + by < size]
    return lax.ppermute(shard, axis, pairs)


def right_rims(pressure, density):
    return shifted((pressure[:, :1], density[:, :1]), "range", -1)


def lower_rims(pressure, density):
    return shifted((pressure[:1], density[:1]), "depth", -1)


def left_rims(column):
    return shifted(column, "range", 1)


def upper_rims(row):
    return shifted(row, "depth", 1)


def shards(
    pressure,
    vel_range,
    vel_depth,
    sound_speed,
    density,
    ahead_speed,
    ahead_density,
    shifts,
    sources,
    wavelet,
):
    height, breadth = pressure.shape
    at_end = lax.axis_index("range") == lax.axis_size("range") - 1
    at_bottom = lax.axis_index("depth") == lax.axis_size("depth") - 1
    col_start = lax.axis_index("range") * breadth
    row_start = lax.axis_index("depth") * height
    full_range = breadth * lax.axis_size("range")
    offset = jnp.int32(0)
    depth_onehot = (
        (sources[:, 0] - row_start)[:, None] == jnp.arange(height, dtype=jnp.int32)[None, :]
    ).astype(jnp.float32)
    extra = ahead_speed.shape[1]
    spread = breadth + extra
    zero_cols = jnp.zeros((height, extra), jnp.float32)
    pressure = jnp.concatenate([pressure, zero_cols], 1)
    vel_range = jnp.concatenate([vel_range, zero_cols], 1)
    vel_depth = jnp.concatenate([vel_depth, zero_cols], 1)
    sound_speed = jnp.concatenate([sound_speed, ahead_speed], 1)
    density = jnp.concatenate([density, ahead_density], 1)
    local_index = jnp.arange(spread, dtype=jnp.int32)
    abs_col = col_start + local_index
    usable = jnp.logical_or(at_end, local_index < breadth)
    inner_edge = jnp.logical_and(local_index == breadth - 1, jnp.logical_not(at_end))
    stiffness = density * sound_speed * sound_speed
    for segment in range(ITERS):
        live = jnp.logical_and(
            usable, jnp.logical_and(abs_col >= offset, abs_col < offset + full_range)
        )
        right_p, right_rho = right_rims(pressure, density)
        p_right = jnp.concatenate([pressure[:, 1:], jnp.zeros_like(pressure[:, :1])], 1)
        p_right = jnp.where(inner_edge[None, :], right_p, p_right)
        rho_right = jnp.concatenate([density[:, 1:], density[:, -1:]], 1)
        rho_right = jnp.where(inner_edge[None, :], right_rho, rho_right)
        rho_right = jnp.where((abs_col == offset + full_range - 1)[None, :], density, rho_right)
        fresh = vel_range - TIME_STEP * (2.0 / (density + rho_right)) * (p_right - pressure)
        vel_range = jnp.where(live[None, :], fresh, vel_range)
        lower_p, lower_rho = lower_rims(pressure, density)
        lower_rho = jnp.where(at_bottom, density[-1:], lower_rho)
        p_lower = jnp.concatenate([pressure[1:], lower_p], 0)
        rho_lower = jnp.concatenate([density[1:], lower_rho], 0)
        fresh = vel_depth - TIME_STEP * (2.0 / (density + rho_lower)) * (p_lower - pressure)
        vel_depth = jnp.where(live[None, :], fresh, vel_depth)
        left_edge = left_rims(vel_range[:, breadth - 1 : breadth])
        range_left = jnp.concatenate([left_edge, vel_range[:, :-1]], 1)
        range_left = jnp.where((abs_col == offset)[None, :], 0.0, range_left)
        upper_edge = upper_rims(vel_depth[-1:])
        depth_upper = jnp.concatenate([upper_edge, vel_depth[:-1]], 0)
        fresh = pressure - TIME_STEP * stiffness * (
            vel_range - range_left + (vel_depth - depth_upper)
        )
        amplitude = wavelet[:, segment]
        range_onehot = jnp.logical_and(
            sources[:, 1][:, None] == abs_col[None, :], usable[None, :]
        ).astype(jnp.float32)
        fresh = fresh + jnp.dot(
            (depth_onehot * amplitude[:, None]).T, range_onehot, precision=lax.Precision.HIGHEST
        )
        pressure = jnp.where(live[None, :], fresh, pressure)
        offset = offset + shifts[segment]
    tails = shifted((pressure[:, :extra], vel_range[:, :extra], vel_depth[:, :extra]), "range", -1)
    finals = []
    for field, tail in zip((pressure, vel_range, vel_depth), tails):
        after = jnp.where(at_end, field[:, breadth:], tail)
        joined = jnp.concatenate([field[:, :breadth], after], 1)
        finals.append(lax.dynamic_slice_in_dim(joined, offset, breadth, 1))
    return (finals[0], finals[1], finals[2])


def solution(mesh):
    placed = (
        P("depth", "range"),
        P("depth", "range"),
        P("depth", "range"),
        P("depth", "range"),
        P("depth", "range"),
        P("depth", None),
        P("depth", None),
        P(),
        P(),
        P(),
    )
    return jax.shard_map(
        shards,
        mesh=mesh,
        in_specs=placed,
        out_specs=(P("depth", "range"), P("depth", "range"), P("depth", "range")),
        check_vma=False,
    )
```

profile of v0, /device:TPU:1, one launch (start us, length us, event | category | flops | bytes accessed | tf_op | source)
XLA Modules:
  0.0 140.5 jit_solution(2661645168777993345)
XLA Ops:
  1.9 2.1 %collective-permute-start.4 = (f32[1,192]{0,1:T(8,128)S(1)}, f32[1,192]{0,1:T(8,128)}, u32[]{:S(2)}, u32[]{:S(2)}) collective-permute-start(f32[1,192]{0,1:T(8,128)S(1)} %pad_slice_fusion.4), channel_id=1, source_target_pairs={{1,0},{2,1},{3,2},{5,4},{6,5},{7,6},{9,8},{10,9},{11,10},{13,12},{... | collective-permute-start | bytes 2312 | tf_op jit(solution)/shard_map/ppermute | solution.py:15
  5.3 1.9 %collective-permute-start.3 = (f32[1,192]{0,1:T(8,128)S(1)}, f32[1,192]{0,1:T(8,128)S(1)}, u32[]{:S(2)}, u32[]{:S(2)}) collective-permute-start(f32[1,192]{0,1:T(8,128)S(1)} %fusion.45), channel_id=1, source_target_pairs={{1,0},{2,1},{3,2},{5,4},{6,5},{7,6},{9,8},{10,9},{11,10},{13,12},{... | collective-permute-start | bytes 2312 | tf_op jit(solution)/shard_map/ppermute | solution.py:15
  7.2 1.3 collective-permute-start.1
  8.5 1.3 collective-permute-start
  19.3 3.1 %subtract_select_fusion.6 = (f32[1024,192]{0,1:T(8,128)S(1)}, f32[1024,192]{0,1:T(8,128)}, f32[1024,192]{0,1:T(8,128)}) fusion(f32[1024,128]{0,1:T(8,128)S(1)} %copy.21, f32[1,192]{0,1:T(8,128)} %collective-permute-done.4, f32[1023,192]{0,1:T(8,128)S(1)} %copy-done.16, f32[1024,128]{0,1:T(8,128)} %copy.25, pred[192]{0:T(512)(128)(4,1)S(1)} %and_and_fusion, ...), kind=kLoop, calls=%fused_computation.28 | loop fusion | flops 2752512 | bytes 6553792 | tf_op jit(solution)/shard_map/jit(_where)/select_n | solution.py:86
  22.4 4.5 %collective-permute-start.5 = (f32[1,192]{0,1:T(8,128)S(1)}, f32[1,192]{0,1:T(8,128)}, u32[]{:S(2)}, u32[]{:S(2)}) collective-permute-start(f32[1,192]{0,1:T(8,128)S(1)} %slice.259), channel_id=1, source_target_pairs={{0,1},{1,2},{2,3},{4,5},{5,6},{6,7},{8,9},{9,10},{10,11},{12,13},{... | collective-permute-start | bytes 2312 | tf_op jit(solution)/shard_map/ppermute | solution.py:15
  28.2 6.3 %collective-permute-done = f32[1024,1]{1,0:T(8,128)} collective-permute-done((f32[1024,1]{1,0:T(8,128)}, f32[1024,1]{1,0:T(8,128)}, u32[]{:S(2)}, u32[]{:S(2)}) %collective-permute-start) | collective-permute-done | bytes 4128 | tf_op jit(solution)/shard_map/ppermute | solution.py:15
  35.7 1.5 %subtract_select_fusion.7 = f32[1024,192]{0,1:T(8,128)S(1)} fusion(f32[1024,128]{0,1:T(8,128)S(1)} %copy.21, f32[1024,191]{0,1:T(8,128)} %get-tuple-element.34, f32[1024,128]{0,1:T(8,128)S(1)} %copy.24, f32[1024]{0:T(1024)S(1)} %reduce.1, pred[192]{0:T(512)(128)(4,1)S(1)} %get-tuple-element.36, pred[192]{0:T(512)(128)(4,1)S(1)} %get-tuple-element.37, ...), kind=kLoop, calls=%fused_computation.29 | loop fusion | flops 2359296 | bytes 4198976 | tf_op jit(solution)/shard_map/jit(_where)/select_n | solution.py:80
  38.1 4.5 %collective-permute-start.2 = (f32[1024,1]{0,1:T(1,128)S(1)}, f32[1024,1]{0,1:T(1,128)S(1)}, u32[]{:S(2)}, u32[]{:S(2)}) collective-permute-start(f32[1024,1]{0,1:T(1,128)S(1)} %slice.251), channel_id=1, source_target_pairs={{0,4},{4,8},{8,12},{12,16},{16,20},{20,24},{24,28},{1,5},{5,9},{9,... | collective-permute-start | bytes 12296 | tf_op jit(solution)/shard_map/ppermute | solution.py:15
  44.6 2.9 %fusion.3 = f32[1024,192]{0,1:T(8,128)S(1)} fusion(f32[1024,128]{0,1:T(8,128)S(1)} %copy.21, f32[1024,192]{0,1:T(8,128)} %get-tuple-element.17, f32[1024,192]{0,1:T(8,128)} %copy-done.11, f32[1024,191]{0,1:T(8,128)} %bitcast.33, f32[1024,1]{0,1:T(1,128)S(1)} %collective-permute-done.2, f32[1024,192]{0,1:T(8,128)} %copy-done.5, f32[1023,192]{0,1:T(8,128)} %bitcast.30, ...), kind=kOutput, calls=%fused_computation.12 | convolution fusion | flops 20859904 | bytes 5244320 | tf_op jit(solution)/shard_map/dot_general | solution.py:99
  47.5 2.1 %collective-permute-start.8 = (f32[1,192]{0,1:T(8,128)S(1)}, f32[1,192]{0,1:T(8,128)S(1)}, u32[]{:S(2)}, u32[]{:S(2)}) collective-permute-start(f32[1,192]{0,1:T(8,128)S(1)} %slice.266), channel_id=1, source_target_pairs={{1,0},{2,1},{3,2},{5,4},{6,5},{7,6},{9,8},{10,9},{11,10},{13,12},{... | collective-permute-start | bytes 2312 | tf_op jit(solution)/shard_map/ppermute | solution.py:15
  49.6 1.3 collective-permute-start.6
  51.9 2.6 %collective-permute-done.8 = f32[1,192]{0,1:T(8,128)S(1)} collective-permute-done((f32[1,192]{0,1:T(8,128)S(1)}, f32[1,192]{0,1:T(8,128)S(1)}, u32[]{:S(2)}, u32[]{:S(2)}) %collective-permute-start.8) | collective-permute-done | bytes 800 | tf_op jit(solution)/shard_map/ppermute | solution.py:15
  54.6 1.5 %subtract_select_fusion.4 = (f32[1024,192]{0,1:T(8,128)}, f32[1024,192]{0,1:T(8,128)S(1)}) fusion(f32[1024,192]{0,1:T(8,128)S(1)} %copy-done.6, f32[1024,192]{0,1:T(8,128)S(1)} %copy-done.13, f32[1024,192]{0,1:T(8,128)S(1)} %fusion.3, f32[1,192]{0,1:T(8,128)S(1)} %collective-permute-done.8, f32[1023,192]{0,1:T(8,128)S(1)} %slice.265, ...), kind=kLoop, calls=%fused_computation.25 | loop fusion | flops 3342336 | bytes 7868992 | tf_op jit(solution)/shard_map/jit(_where)/select_n | solution.py:86
  57.0 4.3 %collective-permute-start.7 = (f32[1024,1]{0,1:T(1,128)S(1)}, f32[1024,1]{0,1:T(1,128)S(1)}, u32[]{:S(2)}, u32[]{:S(2)}) collective-permute-start(f32[1024,1]{0,1:T(1,128)S(1)} %slice.263), channel_id=1, source_target_pairs={{0,4},{4,8},{8,12},{12,16},{16,20},{20,24},{24,28},{1,5},{5,9},{9,... | collective-permute-start | bytes 12296 | tf_op jit(solution)/shard_map/ppermute | solution.py:15
  62.3 5.9 %collective-permute-start.9 = (f32[1,192]{0,1:T(8,128)S(1)}, f32[1,192]{0,1:T(8,128)S(1)}, u32[]{:S(2)}, u32[]{:S(2)}) collective-permute-start(f32[1,192]{0,1:T(8,128)S(1)} %slice.267), channel_id=1, source_target_pairs={{0,1},{1,2},{2,3},{4,5},{5,6},{6,7},{8,9},{9,10},{10,11},{12,13},{... | collective-permute-start | bytes 2312 | tf_op jit(solution)/shard_map/ppermute | solution.py:15
  70.0 2.9 %fusion.2 = f32[1024,192]{0,1:T(8,128)S(1)} fusion(f32[1024,192]{0,1:T(8,128)S(1)} %fusion.3, f32[1024,192]{0,1:T(8,128)} %get-tuple-element.17, f32[1024,192]{0,1:T(8,128)} %copy-done.9, f32[1024,191]{0,1:T(8,128)} %bitcast.32, f32[1024,1]{0,1:T(1,128)S(1)} %collective-permute-done.7, f32[1024,192]{0,1:T(8,128)} %get-tuple-element.15, ...), kind=kOutput, calls=%fused_computation.10 | convolution fusion | flops 20859904 | bytes 5506464 | tf_op jit(solution)/shard_map/dot_general | solution.py:99
  72.9 1.9 %collective-permute-start.12 = (f32[1,192]{0,1:T(8,128)S(1)}, f32[1,192]{0,1:T(8,128)S(1)}, u32[]{:S(2)}, u32[]{:S(2)}) collective-permute-start(f32[1,192]{0,1:T(8,128)S(1)} %slice.274), channel_id=1, source_target_pairs={{1,0},{2,1},{3,2},{5,4},{6,5},{7,6},{9,8},{10,9},{11,10},{13,12},{... | collective-permute-start | bytes 2312 | tf_op jit(solution)/shard_map/ppermute | solution.py:15
  74.9 1.3 collective-permute-start.10
  76.6 2.7 %collective-permute-done.12 = f32[1,192]{0,1:T(8,128)S(1)} collective-permute-done((f32[1,192]{0,1:T(8,128)S(1)}, f32[1,192]{0,1:T(8,128)S(1)}, u32[]{:S(2)}, u32[]{:S(2)}) %collective-permute-start.12) | collective-permute-done | bytes 800 | tf_op jit(solution)/shard_map/ppermute | solution.py:15
  79.3 2.6 %subtract_select_fusion.2 = (f32[1024,192]{0,1:T(8,128)}, f32[1024,192]{0,1:T(8,128)S(1)}) fusion(f32[1024,192]{0,1:T(8,128)} %get-tuple-element.15, f32[1024,192]{0,1:T(8,128)S(1)} %copy-done.14, f32[1024,192]{0,1:T(8,128)S(1)} %fusion.2, f32[1,192]{0,1:T(8,128)S(1)} %collective-permute-done.12, f32[1023,192]{0,1:T(8,128)S(1)} %slice.273, ...), kind=kLoop, calls=%fused_computation.22 | loop fusion | flops 3342336 | bytes 7868992 | tf_op jit(solution)/shard_map/jit(_where)/select_n | solution.py:86
  82.8 3.2 %collective-permute-start.11 = (f32[1024,1]{0,1:T(1,128)S(1)}, f32[1024,1]{0,1:T(1,128)S(1)}, u32[]{:S(2)}, u32[]{:S(2)}) collective-permute-start(f32[1024,1]{0,1:T(1,128)S(1)} %slice.271), channel_id=1, source_target_pairs={{0,4},{4,8},{8,12},{12,16},{16,20},{20,24},{24,28},{1,5},{5,9},{9,... | collective-permute-start | bytes 12296 | tf_op jit(solution)/shard_map/ppermute | solution.py:15
  87.0 5.5 %collective-permute-start.13 = (f32[1,192]{0,1:T(8,128)S(1)}, f32[1,192]{0,1:T(8,128)S(1)}, u32[]{:S(2)}, u32[]{:S(2)}) collective-permute-start(f32[1,192]{0,1:T(8,128)S(1)} %slice.275), channel_id=1, source_target_pairs={{0,1},{1,2},{2,3},{4,5},{5,6},{6,7},{8,9},{9,10},{10,11},{12,13},{... | collective-permute-start | bytes 2312 | tf_op jit(solution)/shard_map/ppermute | solution.py:15
  94.1 2.9 %fusion.1 = f32[1024,192]{0,1:T(8,128)S(1)} fusion(f32[1024,192]{0,1:T(8,128)S(1)} %fusion.2, f32[1024,192]{0,1:T(8,128)} %get-tuple-element.17, f32[1024,192]{0,1:T(8,128)} %copy-done.7, f32[1024,191]{0,1:T(8,128)} %bitcast.31, f32[1024,1]{0,1:T(1,128)S(1)} %collective-permute-done.11, f32[1024,192]{0,1:T(8,128)} %get-tuple-element.13, ...), kind=kOutput, calls=%fused_computation.8 | convolution fusion | flops 20859904 | bytes 5506464 | tf_op jit(solution)/shard_map/dot_general | solution.py:99
  97.0 1.9 %collective-permute-start.16 = (f32[1,192]{0,1:T(8,128)S(1)}, f32[1,192]{0,1:T(8,128)S(1)}, u32[]{:S(2)}, u32[]{:S(2)}) collective-permute-start(f32[1,192]{0,1:T(8,128)S(1)} %slice.282), channel_id=1, source_target_pairs={{1,0},{2,1},{3,2},{5,4},{6,5},{7,6},{9,8},{10,9},{11,10},{13,12},{... | collective-permute-start | bytes 2312 | tf_op jit(solution)/shard_map/ppermute | solution.py:15
  100.7 3.0 %collective-permute-done.16 = f32[1,192]{0,1:T(8,128)S(1)} collective-permute-done((f32[1,192]{0,1:T(8,128)S(1)}, f32[1,192]{0,1:T(8,128)S(1)}, u32[]{:S(2)}, u32[]{:S(2)}) %collective-permute-start.16) | collective-permute-done | bytes 800 | tf_op jit(solution)/shard_map/ppermute | solution.py:15
  103.7 2.6 %subtract_select_fusion = (f32[1024,192]{0,1:T(8,128)S(1)}, f32[1024,192]{0,1:T(8,128)}) fusion(f32[1024,192]{0,1:T(8,128)} %get-tuple-element.13, f32[1024,192]{0,1:T(8,128)S(1)} %copy-done.15, f32[1024,192]{0,1:T(8,128)S(1)} %fusion.1, f32[1,192]{0,1:T(8,128)S(1)} %collective-permute-done.16, f32[1023,192]{0,1:T(8,128)S(1)} %slice.281, ...), kind=kLoop, calls=%fused_computation.19 | loop fusion | flops 3342336 | bytes 7868992 | tf_op jit(solution)/shard_map/jit(_where)/select_n | solution.py:86
  107.0 3.6 %collective-permute-start.15 = (f32[1024,1]{0,1:T(1,128)S(1)}, f32[1024,1]{0,1:T(1,128)S(1)}, u32[]{:S(2)}, u32[]{:S(2)}) collective-permute-start(f32[1024,1]{0,1:T(1,128)S(1)} %slice.279), channel_id=1, source_target_pairs={{0,4},{4,8},{8,12},{12,16},{16,20},{20,24},{24,28},{1,5},{5,9},{9,... | collective-permute-start | bytes 12296 | tf_op jit(solution)/shard_map/ppermute | solution.py:15
  110.7 5.7 %collective-permute-start.17 = (f32[1,192]{0,1:T(8,128)S(1)}, f32[1,192]{0,1:T(8,128)S(1)}, u32[]{:S(2)}, u32[]{:S(2)}) collective-permute-start(f32[1,192]{0,1:T(8,128)S(1)} %slice.283), channel_id=1, source_target_pairs={{0,1},{1,2},{2,3},{4,5},{5,6},{6,7},{8,9},{9,10},{10,11},{12,13},{... | collective-permute-start | bytes 2312 | tf_op jit(solution)/shard_map/ppermute | solution.py:15
  122.6 2.2 %fusion = f32[1024,192]{0,1:T(8,128)S(1)} fusion(f32[1024,192]{0,1:T(8,128)S(1)} %fusion.1, f32[1024,192]{0,1:T(8,128)S(1)} %copy-done.4, f32[1024,192]{0,1:T(8,128)} %get-tuple-element.12, f32[1024,191]{0,1:T(8,128)} %bitcast.27, f32[1024,1]{0,1:T(1,128)S(1)} %collective-permute-done.15, f32[1024,192]{0,1:T(8,128)S(1)} %get-tuple-element.11, ...), kind=kOutput, calls=%fused_computation.6 | convolution fusion | flops 20859904 | bytes 5506464 | tf_op jit(solution)/shard_map/dot_general | solution.py:99
  126.8 3.5 %collective-permute-done.19 = f32[1024,64]{0,1:T(8,128)S(1)} collective-permute-done((f32[1024,64]{0,1:T(8,128)S(1)}, f32[1024,64]{0,1:T(8,128)S(1)}, u32[]{:S(2)}, u32[]{:S(2)}) %collective-permute-start.19) | collective-permute-done | bytes 262176 | tf_op jit(solution)/shard_map/ppermute | solution.py:15
  132.4 3.4 %collective-permute-done.20 = f32[1024,64]{0,1:T(8,128)} collective-permute-done((f32[1024,64]{0,1:T(8,128)}, f32[1024,64]{0,1:T(8,128)}, u32[]{:S(2)}, u32[]{:S(2)}) %collective-permute-start.20) | collective-permute-done | bytes 262176 | tf_op jit(solution)/shard_map/ppermute | solution.py:15
  (131 shorter events, 39.4 us)
Async XLA Ops:
  1.9 3.3 %copy-start = (f32[1024,64]{0,1:T(8,128)S(1)}, f32[1024,64]{0,1:T(8,128)}, u32[]{:S(2)}) copy-start(f32[1024,64]{0,1:T(8,128)} %param.16) | copy-start | bytes 786436
  1.9 16.3 %collective-permute-start.4 = (f32[1,192]{0,1:T(8,128)S(1)}, f32[1,192]{0,1:T(8,128)}, u32[]{:S(2)}, u32[]{:S(2)}) collective-permute-start(f32[1,192]{0,1:T(8,128)S(1)} %pad_slice_fusion.4), channel_id=1, source_target_pairs={{1,0},{2,1},{3,2},{5,4},{6,5},{7,6},{9,8},{10,9},{11,10},{13,12},{... | collective-permute-start | bytes 2312 | tf_op jit(solution)/shard_map/ppermute | solution.py:15
  5.3 12.9 %collective-permute-start.3 = (f32[1,192]{0,1:T(8,128)S(1)}, f32[1,192]{0,1:T(8,128)S(1)}, u32[]{:S(2)}, u32[]{:S(2)}) collective-permute-start(f32[1,192]{0,1:T(8,128)S(1)} %fusion.45), channel_id=1, source_target_pairs={{1,0},{2,1},{3,2},{5,4},{6,5},{7,6},{9,8},{10,9},{11,10},{13,12},{... | collective-permute-start | bytes 2312 | tf_op jit(solution)/shard_map/ppermute | solution.py:15
  7.2 19.7 %collective-permute-start.1 = (f32[1024,1]{1,0:T(8,128)}, f32[1024,1]{1,0:T(8,128)}, u32[]{:S(2)}, u32[]{:S(2)}) collective-permute-start(f32[1024,1]{1,0:T(8,128)} %bitcast.19), channel_id=1, source_target_pairs={{4,0},{8,4},{12,8},{16,12},{20,16},{24,20},{28,24},{5,1},{9,5},{13... | collective-permute-start | bytes 12296 | tf_op jit(solution)/shard_map/ppermute | solution.py:15
  8.5 26.0 %collective-permute-start = (f32[1024,1]{1,0:T(8,128)}, f32[1024,1]{1,0:T(8,128)}, u32[]{:S(2)}, u32[]{:S(2)}) collective-permute-start(f32[1024,1]{1,0:T(8,128)} %bitcast.20), channel_id=1, source_target_pairs={{4,0},{8,4},{12,8},{16,12},{20,16},{24,20},{28,24},{5,1},{9,5},{13... | collective-permute-start | bytes 12296 | tf_op jit(solution)/shard_map/ppermute | solution.py:15
  12.1 3.8 %copy-start.17 = (f32[1024,128]{1,0:T(8,128)S(1)}, f32[1024,128]{1,0:T(8,128)}, u32[]{:S(2)}) copy-start(f32[1024,128]{1,0:T(8,128)} %param.12) | copy-start | bytes 1572868
  13.1 41.5 %copy-start.1 = (f32[1024,191]{0,1:T(8,128)}, f32[1024,191]{0,1:T(8,128)S(1)}, u32[]{:S(2)}) copy-start(f32[1024,191]{0,1:T(8,128)S(1)} %get-tuple-element.35) | copy-start | bytes 2347012
  22.3 14.9 %copy-start.5 = (f32[1024,192]{0,1:T(8,128)}, f32[1024,192]{0,1:T(8,128)S(1)}, u32[]{:S(2)}) copy-start(f32[1024,192]{0,1:T(8,128)S(1)} %get-tuple-element.9) | copy-start | bytes 2359300
  22.4 21.5 %collective-permute-start.5 = (f32[1,192]{0,1:T(8,128)S(1)}, f32[1,192]{0,1:T(8,128)}, u32[]{:S(2)}, u32[]{:S(2)}) collective-permute-start(f32[1,192]{0,1:T(8,128)S(1)} %slice.259), channel_id=1, source_target_pairs={{0,1},{1,2},{2,3},{4,5},{5,6},{6,7},{8,9},{9,10},{10,11},{12,13},{... | collective-permute-start | bytes 2312 | tf_op jit(solution)/shard_map/ppermute | solution.py:15
  38.1 5.8 %collective-permute-start.2 = (f32[1024,1]{0,1:T(1,128)S(1)}, f32[1024,1]{0,1:T(1,128)S(1)}, u32[]{:S(2)}, u32[]{:S(2)}) collective-permute-start(f32[1024,1]{0,1:T(1,128)S(1)} %slice.251), channel_id=1, source_target_pairs={{0,4},{4,8},{8,12},{12,16},{16,20},{20,24},{24,28},{1,5},{5,9},{9,... | collective-permute-start | bytes 12296 | tf_op jit(solution)/shard_map/ppermute | solution.py:15
  47.5 7.1 %collective-permute-start.8 = (f32[1,192]{0,1:T(8,128)S(1)}, f32[1,192]{0,1:T(8,128)S(1)}, u32[]{:S(2)}, u32[]{:S(2)}) collective-permute-start(f32[1,192]{0,1:T(8,128)S(1)} %slice.266), channel_id=1, source_target_pairs={{1,0},{2,1},{3,2},{5,4},{6,5},{7,6},{9,8},{10,9},{11,10},{13,12},{... | collective-permute-start | bytes 2312 | tf_op jit(solution)/shard_map/ppermute | solution.py:15
  49.6 5.0 %collective-permute-start.6 = (f32[1024,1]{0,1:T(1,128)S(1)}, f32[1024,1]{0,1:T(1,128)S(1)}, u32[]{:S(2)}, u32[]{:S(2)}) collective-permute-start(f32[1024,1]{0,1:T(1,128)S(1)} %slice.261), channel_id=1, source_target_pairs={{4,0},{8,4},{12,8},{16,12},{20,16},{24,20},{28,24},{5,1},{9,5},{13... | collective-permute-start | bytes 12296 | tf_op jit(solution)/shard_map/ppermute | solution.py:15
  51.6 3.0 %copy-start.13 = (f32[1024,192]{0,1:T(8,128)S(1)}, f32[1024,192]{0,1:T(8,128)}, u32[]{:S(2)}) copy-start(f32[1024,192]{0,1:T(8,128)} %get-tuple-element.10) | copy-start | bytes 2359300
  57.0 13.0 %collective-permute-start.7 = (f32[1024,1]{0,1:T(1,128)S(1)}, f32[1024,1]{0,1:T(1,128)S(1)}, u32[]{:S(2)}, u32[]{:S(2)}) collective-permute-start(f32[1024,1]{0,1:T(1,128)S(1)} %slice.263), channel_id=1, source_target_pairs={{0,4},{4,8},{8,12},{12,16},{16,20},{20,24},{24,28},{1,5},{5,9},{9,... | collective-permute-start | bytes 12296 | tf_op jit(solution)/shard_map/ppermute | solution.py:15
  62.3 7.7 %collective-permute-start.9 = (f32[1,192]{0,1:T(8,128)S(1)}, f32[1,192]{0,1:T(8,128)S(1)}, u32[]{:S(2)}, u32[]{:S(2)}) collective-permute-start(f32[1,192]{0,1:T(8,128)S(1)} %slice.267), channel_id=1, source_target_pairs={{0,1},{1,2},{2,3},{4,5},{5,6},{6,7},{8,9},{9,10},{10,11},{12,13},{... | collective-permute-start | bytes 2312 | tf_op jit(solution)/shard_map/ppermute | solution.py:15
  72.9 6.4 %collective-permute-start.12 = (f32[1,192]{0,1:T(8,128)S(1)}, f32[1,192]{0,1:T(8,128)S(1)}, u32[]{:S(2)}, u32[]{:S(2)}) collective-permute-start(f32[1,192]{0,1:T(8,128)S(1)} %slice.274), channel_id=1, source_target_pairs={{1,0},{2,1},{3,2},{5,4},{6,5},{7,6},{9,8},{10,9},{11,10},{13,12},{... | collective-permute-start | bytes 2312 | tf_op jit(solution)/shard_map/ppermute | solution.py:15
  74.9 4.5 %collective-permute-start.10 = (f32[1024,1]{0,1:T(1,128)S(1)}, f32[1024,1]{0,1:T(1,128)S(1)}, u32[]{:S(2)}, u32[]{:S(2)}) collective-permute-start(f32[1024,1]{0,1:T(1,128)S(1)} %slice.269), channel_id=1, source_target_pairs={{4,0},{8,4},{12,8},{16,12},{20,16},{24,20},{28,24},{5,1},{9,5},{13... | collective-permute-start | bytes 12296 | tf_op jit(solution)/shard_map/ppermute | solution.py:15
  76.2 3.1 %copy-start.14 = (f32[1024,192]{0,1:T(8,128)S(1)}, f32[1024,192]{0,1:T(8,128)}, u32[]{:S(2)}) copy-start(f32[1024,192]{0,1:T(8,128)} %get-tuple-element.10) | copy-start | bytes 2359300
  76.5 2.9 %copy-start.2 = (f32[1024,191]{0,1:T(8,128)S(1)}, f32[1024,191]{0,1:T(8,128)}, u32[]{:S(2)}) copy-start(f32[1024,191]{0,1:T(8,128)} %copy-done.1) | copy-start | bytes 2347012
  82.8 11.3 %collective-permute-start.11 = (f32[1024,1]{0,1:T(1,128)S(1)}, f32[1024,1]{0,1:T(1,128)S(1)}, u32[]{:S(2)}, u32[]{:S(2)}) collective-permute-start(f32[1024,1]{0,1:T(1,128)S(1)} %slice.271), channel_id=1, source_target_pairs={{0,4},{4,8},{8,12},{12,16},{16,20},{20,24},{24,28},{1,5},{5,9},{9,... | collective-permute-start | bytes 12296 | tf_op jit(solution)/shard_map/ppermute | solution.py:15
  87.0 7.1 %collective-permute-start.13 = (f32[1,192]{0,1:T(8,128)S(1)}, f32[1,192]{0,1:T(8,128)S(1)}, u32[]{:S(2)}, u32[]{:S(2)}) collective-permute-start(f32[1,192]{0,1:T(8,128)S(1)} %slice.275), channel_id=1, source_target_pairs={{0,1},{1,2},{2,3},{4,5},{5,6},{6,7},{8,9},{9,10},{10,11},{12,13},{... | collective-permute-start | bytes 2312 | tf_op jit(solution)/shard_map/ppermute | solution.py:15
  97.0 6.6 %collective-permute-start.16 = (f32[1,192]{0,1:T(8,128)S(1)}, f32[1,192]{0,1:T(8,128)S(1)}, u32[]{:S(2)}, u32[]{:S(2)}) collective-permute-start(f32[1,192]{0,1:T(8,128)S(1)} %slice.282), channel_id=1, source_target_pairs={{1,0},{2,1},{3,2},{5,4},{6,5},{7,6},{9,8},{10,9},{11,10},{13,12},{... | collective-permute-start | bytes 2312 | tf_op jit(solution)/shard_map/ppermute | solution.py:15
  99.0 4.7 %collective-permute-start.14 = (f32[1024,1]{0,1:T(1,128)S(1)}, f32[1024,1]{0,1:T(1,128)S(1)}, u32[]{:S(2)}, u32[]{:S(2)}) collective-permute-start(f32[1024,1]{0,1:T(1,128)S(1)} %slice.277), channel_id=1, source_target_pairs={{4,0},{8,4},{12,8},{16,12},{20,16},{24,20},{28,24},{5,1},{9,5},{13... | collective-permute-start | bytes 12296 | tf_op jit(solution)/shard_map/ppermute | solution.py:15
  100.3 3.4 %copy-start.15 = (f32[1024,192]{0,1:T(8,128)S(1)}, f32[1024,192]{0,1:T(8,128)}, u32[]{:S(2)}) copy-start(f32[1024,192]{0,1:T(8,128)} %get-tuple-element.10) | copy-start | bytes 2359300
  100.6 3.1 %copy-start.3 = (f32[1024,191]{0,1:T(8,128)S(1)}, f32[1024,191]{0,1:T(8,128)}, u32[]{:S(2)}) copy-start(f32[1024,191]{0,1:T(8,128)} %copy-done.1) | copy-start | bytes 2347012
  100.6 3.1 %copy-start.8 = (f32[1024,192]{0,1:T(8,128)S(1)}, f32[1024,192]{0,1:T(8,128)}, u32[]{:S(2)}) copy-start(f32[1024,192]{0,1:T(8,128)} %copy-done.7) | copy-start | bytes 2359300
  107.0 15.5 %collective-permute-start.15 = (f32[1024,1]{0,1:T(1,128)S(1)}, f32[1024,1]{0,1:T(1,128)S(1)}, u32[]{:S(2)}, u32[]{:S(2)}) collective-permute-start(f32[1024,1]{0,1:T(1,128)S(1)} %slice.279), channel_id=1, source_target_pairs={{0,4},{4,8},{8,12},{12,16},{16,20},{20,24},{24,28},{1,5},{5,9},{9,... | collective-permute-start | bytes 12296 | tf_op jit(solution)/shard_map/ppermute | solution.py:15
  110.7 11.8 %collective-permute-start.17 = (f32[1,192]{0,1:T(8,128)S(1)}, f32[1,192]{0,1:T(8,128)S(1)}, u32[]{:S(2)}, u32[]{:S(2)}) collective-permute-start(f32[1,192]{0,1:T(8,128)S(1)} %slice.283), channel_id=1, source_target_pairs={{0,1},{1,2},{2,3},{4,5},{5,6},{6,7},{8,9},{9,10},{10,11},{12,13},{... | collective-permute-start | bytes 2312 | tf_op jit(solution)/shard_map/ppermute | solution.py:15
  119.2 3.4 %copy-start.4 = (f32[1024,192]{0,1:T(8,128)S(1)}, f32[1024,192]{0,1:T(8,128)}, u32[]{:S(2)}) copy-start(f32[1024,192]{0,1:T(8,128)} %get-tuple-element.17) | copy-start | bytes 2359300
  119.9 10.3 %collective-permute-start.19 = (f32[1024,64]{0,1:T(8,128)S(1)}, f32[1024,64]{0,1:T(8,128)S(1)}, u32[]{:S(2)}, u32[]{:S(2)}) collective-permute-start(f32[1024,64]{0,1:T(8,128)S(1)} %slice.290), channel_id=1, source_target_pairs={{4,0},{8,4},{12,8},{16,12},{20,16},{24,20},{28,24},{5,1},{9,5},{13... | collective-permute-start | bytes 786440 | tf_op jit(solution)/shard_map/ppermute | solution.py:15
  121.2 14.5 %collective-permute-start.20 = (f32[1024,64]{0,1:T(8,128)}, f32[1024,64]{0,1:T(8,128)}, u32[]{:S(2)}, u32[]{:S(2)}) collective-permute-start(f32[1024,64]{0,1:T(8,128)} %slice.293), channel_id=1, source_target_pairs={{4,0},{8,4},{12,8},{16,12},{20,16},{24,20},{28,24},{5,1},{9,5},{13... | collective-permute-start | bytes 786440 | tf_op jit(solution)/shard_map/ppermute | solution.py:15
  125.5 12.8 %collective-permute-start.18 = (f32[1024,64]{0,1:T(8,128)}, f32[1024,64]{0,1:T(8,128)}, u32[]{:S(2)}, u32[]{:S(2)}) collective-permute-start(f32[1024,64]{0,1:T(8,128)} %slice.287), channel_id=1, source_target_pairs={{4,0},{8,4},{12,8},{16,12},{20,16},{24,20},{28,24},{5,1},{9,5},{13... | collective-permute-start | bytes 786440 | tf_op jit(solution)/shard_map/ppermute | solution.py:15
  (14 other events, 17.9 us)
where the time goes:
time: 142 us; the launch traced here: 140 us
  starting transfers between devices  57.5 us (40%)
  local copies, waits for them, and re-layouts  22.9 us (16%)
  waiting for transfers between devices  22.9 us (16%)
  other arithmetic  21.3 us (15%)
  matrix products  10.8 us (8%)
  between operations  5.17 us (4%)
    ppermute x21, starting transfers between devices, shifted(): return lax.ppermute(shard, axis, pairs)  57.5 us
    ppermute x21, waiting for transfers between devices, shifted(): return lax.ppermute(shard, axis, pairs)  22.9 us
    unnamed x58, local copies, waits for them, and re-layouts  12.8 us
    dot_general x4, matrix products, shards(): jnp.dot((depth_onehot * amplitude[:, None]).T, range_onehot, precision=la...  10.8 us
    select_n x4, other arithmetic, shards(): vel_depth = jnp.where(live[None, :], fresh, vel_depth)  9.74 us
    select_n x3, other arithmetic, shards(): after = jnp.where(at_end, field[:, breadth:], tail)  2.95 us
  transfers between devices with their start and end apart: 21, of which 8 were waited for; matrix products, arithmetic and copies ran while one was open for 22% of the time, Pallas kernels for 0%

commit v1 on v0

v1 whole, which is shorter than its diff:
```python
import functools

import jax
import jax.numpy as jnp
from jax import lax
from jax.experimental import pallas as pl
from jax.experimental.pallas import tpu as pltpu
from jax.sharding import PartitionSpec as P

ITERS = 4
TIME_STEP = 0.6
LANES = 128
TILE = 8
MARGIN = 16
SKEW = 4
WIDTH = 42
GROUPS = 6
BLOCK = 64

FAR = 1 << 20


def lane_ids(rows):
    return lax.broadcasted_iota(jnp.int32, (rows, LANES), 1)


def between(lanes, low, high):
    return jnp.logical_and(lanes >= low, lanes < high)


def roll(x, by):
    return pltpu.roll(x, by % LANES, 1)


def for_rows(start, stop, fn, size=BLOCK):
    whole = (stop - start) // size

    def step(i, carry):
        fn(pl.multiple_of(start + i * size, TILE), size)
        return carry

    if whole > 1:
        lax.fori_loop(0, whole, step, 0)
    elif whole == 1:
        fn(start, size)
    if start + whole * size < stop:
        fn(start + whole * size, stop - start - whole * size)


def offsets_of(shifts):
    found = [jnp.int32(0)]
    for t in range(ITERS):
        found.append(found[-1] + shifts[t])
    return found


def set_coefs(n, c, rho, ax, az, stiff):
    def coefs(r, k):
        here = pl.ds(r, k)
        dense, speed = rho[here, :], c[here, :]
        ax[here, :] = (2.0 * TIME_STEP) / (dense + roll(dense, -1))
        az[here, :] = (2.0 * TIME_STEP) / (dense + rho[pl.ds(r + 1, k), :])
        stiff[here, :] = TIME_STEP * (dense * speed * speed)

    for_rows(0, n - TILE, coefs)


def inject(field, sources, wavelet, t, local_row, first_col, last_lane):
    rows = lax.broadcasted_iota(jnp.int32, (TILE, LANES), 0)
    lanes = lane_ids(TILE)
    for k in range(sources.shape[0]):
        row, inside = local_row(sources[k, 0])
        lane = sources[k, 1] - first_col
        good = jnp.logical_and(inside, jnp.logical_and(lane >= 0, lane <= last_lane))
        row = jnp.where(good, row, 0)
        amount = jnp.where(good, wavelet[k, t], 0.0)
        at = pl.ds(pl.multiple_of((row // TILE) * TILE, TILE), TILE)
        here = jnp.logical_and(rows == row % TILE, lanes == lane)
        field[at, :] = field[at, :] + jnp.where(here, amount, 0.0)


def left_steps(n, fields, coefs, stages, shifts, sources, wavelet, local_row):
    ax, az, stiff = coefs
    ps, us, ws = stages
    offsets = offsets_of(shifts)
    place = lax.axis_index("range")
    for t in range(ITERS):
        p, u, w = fields if t == 0 else (ps.at[t - 1], us.at[t - 1], ws.at[t - 1])
        u_new, w_new, p_new = us.at[t], ws.at[t], ps.at[t]
        wall = jnp.where(place == 0, offsets[t], -1)

        def speeds(r, k):
            here = pl.ds(r, k)
            now = p[here, :]
            u_new[here, :] = u[here, :] - ax[here, :] * (roll(now, -1) - now)
            w_new[here, :] = w[here, :] - az[here, :] * (p[pl.ds(r + 1, k), :] - now)

        def press(r, k):
            here = pl.ds(r, k)
            fast = u_new[here, :]
            left = jnp.where(lane_ids(k) == wall, 0.0, roll(fast, 1))
            down = w_new[here, :] - w_new[pl.ds(r - 1, k), :]
            p_new[here, :] = p[here, :] - stiff[here, :] * ((fast - left) + down)

        for_rows(0, n - TILE, speeds)
        for_rows(TILE, n - TILE, press)
        inject(p_new, sources, wavelet, t, local_row, place * LANES, LANES - 1)


def slanted(r, k, p0, stages, stiff, rho):
    ps, us, ws = stages
    here = pl.ds(r, k)
    lanes = lane_ids(k)

    def pick(parts):
        found = parts[-1]
        for t in range(len(parts) - 2, -1, -1):
            found = jnp.where(lanes <= t, parts[t], found)
        return found

    a = pick([p0[here, :]] + [ps[t, here, :] for t in range(ITERS - 1)])
    b = pick([us[t, here, :] for t in range(ITERS)])
    c = pick([ws[t, here, :] for t in range(ITERS)])
    found = roll(rho[here, :], 4 * SKEW)
    found = jnp.where(lanes < 4 * SKEW, roll(stiff[here, :], 3 * SKEW), found)
    found = jnp.where(lanes < 3 * SKEW, roll(c, 2 * SKEW), found)
    found = jnp.where(lanes < 2 * SKEW, roll(b, SKEW), found)
    return jnp.where(lanes < SKEW, a, found)


def packed(p, u, w):
    lanes = lane_ids(p.shape[0])
    found = jnp.where(
        between(lanes, SKEW, SKEW + 2 * WIDTH), roll(u, WIDTH), roll(w, 2 * WIDTH)
    )
    return jnp.where(between(lanes, SKEW, SKEW + WIDTH), p, found)


def finals(stages, here):
    return [stage[ITERS - 1, here, :] for stage in stages]


def first_kernel(n, height, *refs):
    shifts, sources, wavelet, p, u, w, c, rho = refs[:8]
    lows = refs[8:13]
    ahead, low_ahead = refs[13:15], refs[15:17]
    plane, done, slant, to_up, to_down = refs[17:22]
    ax, az, stiff = refs[22:25]
    stages = refs[25:]
    for k, (top, low) in enumerate(zip((p, u, w, c, rho), lows)):
        to_up[pl.ds(k * TILE, TILE), :] = top[pl.ds(0, TILE), :]
        to_down[pl.ds(k * TILE, TILE), :] = low[...]
    to_up[pl.ds(5 * TILE, TILE), :] = jnp.concatenate([ref[...] for ref in ahead], 1)
    to_down[pl.ds(5 * TILE, TILE), :] = jnp.concatenate([ref[...] for ref in low_ahead], 1)
    set_coefs(n, c, rho, ax, az, stiff)
    base = lax.axis_index("depth") * height

    def local_row(row):
        row = row - base
        return row, jnp.logical_and(row >= 0, row < n)

    left_steps(n, (p, u, w), (ax, az, stiff), stages, shifts, sources, wavelet, local_row)

    def finish(r, k):
        fields = finals(stages, pl.ds(r, k))
        there = pl.ds(r - MARGIN, k)
        plane[there, :] = packed(*fields)
        for f in range(3):
            done[f, there, :] = fields[f]
        slant[there, :] = slanted(r, k, p, stages, stiff, rho)

    for_rows(MARGIN, n - MARGIN, finish)


def ghost_rows(up, down, k, last_own):
    place = lax.axis_index("depth")
    at = pl.ds(k * TILE, TILE)
    above, below = up[at, :], down[at, :]
    if k == 4:
        above = jnp.where(place == 0, 1.0, above)
        below = jnp.where(place == lax.axis_size("depth") - 1, last_own, below)
    return above, below


def second_kernel(n, height, n_first, *refs):
    shifts, sources, wavelet = refs[:3]
    tops, lows = refs[3:8], refs[8:13]
    up, down, first_slant = refs[13:16]
    plane, done, slant = refs[16:19]
    ax, az, stiff = refs[19:22]
    stages, inner, full = refs[22:25], refs[25:30], refs[30]
    head = 3 * MARGIN
    split = n_first - 2 * MARGIN
    for k in range(5):
        filler = jnp.full((TILE, LANES), 1.0 if k == 4 else 0.0, jnp.float32)
        last_own = jnp.broadcast_to(lows[k][pl.ds(height - split - 1, 1), :], (TILE, LANES))
        above, below = ghost_rows(up, down, k, last_own)
        inner[k][pl.ds(0, TILE), :] = filler
        inner[k][pl.ds(TILE, TILE), :] = above
        inner[k][pl.ds(2 * TILE, 2 * MARGIN), :] = tops[k][...]

        def bring(r, rows, k=k):
            inner[k][pl.ds(r + head, rows), :] = lows[k][pl.ds(r, rows), :]

        for_rows(0, height - split, bring)
        inner[k][pl.ds(n - 2 * TILE, TILE), :] = below
        inner[k][pl.ds(n - TILE, TILE), :] = filler
    p, u, w, c, rho = inner
    set_coefs(n, c, rho, ax, az, stiff)
    place = lax.axis_index("depth")
    at = pl.ds(TILE, TILE)
    az[at, :] = jnp.where(place == 0, 0.0, az[at, :])
    base = place * height

    def local_row(row):
        row = row - base
        low = jnp.logical_and(row >= -TILE, row < 2 * MARGIN)
        high = jnp.logical_and(row >= split, row < height + TILE)
        return jnp.where(low, row + MARGIN, row - split + head), jnp.logical_or(low, high)

    left_steps(n, (p, u, w), (ax, az, stiff), stages, shifts, sources, wavelet, local_row)

    def finish(shift, r, k):
        fields = finals(stages, pl.ds(r, k))
        there = pl.ds(r - shift, k)
        plane[there, :] = packed(*fields)
        for f in range(3):
            done[f, there, :] = fields[f]

    for_rows(MARGIN, 2 * MARGIN, functools.partial(finish, MARGIN))
    for_rows(head + MARGIN, n - MARGIN, functools.partial(finish, head))

    def lean(shift, r, k):
        full[pl.ds(r + shift, k), :] = slanted(r, k, p, stages, stiff, rho)

    def copy(r, k):
        full[pl.ds(r + 2 * MARGIN, k), :] = first_slant[pl.ds(r, k), :]

    for_rows(TILE, 2 * MARGIN, functools.partial(lean, 0))
    for_rows(head + MARGIN, n - TILE, functools.partial(lean, split + MARGIN - head))
    for_rows(0, n_first - 2 * MARGIN, copy)
    ends = jnp.zeros((TILE, LANES), jnp.float32)
    each = (height + 2 * MARGIN) // GROUPS
    full[pl.ds(0, TILE), :] = ends
    full[pl.ds(height + 2 * MARGIN - TILE, TILE), :] = ends

    def gather(r, k):
        lanes = lane_ids(k)
        found = full[pl.ds(r, k), :]
        for g in range(1, GROUPS):
            part = roll(full[pl.ds(r + g * each, k), :], 5 * SKEW * g)
            found = jnp.where(lanes < 5 * SKEW * g, found, part)
        slant[pl.ds(r, k), :] = found

    for_rows(0, each, gather)


def right_kernel(height, n_first, extra, *refs):
    shifts, sources, wavelet = refs[:3]
    own, ahead = refs[3:8], refs[8:10]
    up, down, slant, first_done, second_done = refs[10:15]
    merged, rest = refs[15:17]
    p, u, w, c, rho, ax, az, al, stiff, gp, gu, gw = refs[17:]
    half = LANES - extra
    n = height + 2 * MARGIN
    place, depth = lax.axis_index("range"), lax.axis_index("depth")
    at_end = place == lax.axis_size("range") - 1
    each = n // GROUPS
    offsets = offsets_of(shifts)
    ghosts = (gp, gu, gw, stiff, rho)

    for g in range(GROUPS):

        def spread(r, k, g=g):
            part = slant[pl.ds(r, k), :]
            for f, ghost in enumerate(ghosts):
                ghost[pl.ds(r + g * each, k), :] = roll(part, half - SKEW * f - 5 * SKEW * g)

        for_rows(0, each, spread)

    def place_rows(e, k, parts, ahead_c, ahead_r):
        here = pl.ds(e, k)
        lanes = lane_ids(k)
        mine = lanes < half
        ghost = jnp.logical_and(between(lanes, half, half + SKEW), jnp.logical_not(at_end))
        blank = jnp.zeros((k, half), jnp.float32)
        for ref, part, source in zip((p, u, w), parts, (gp, gu, gw)):
            other = jnp.where(ghost, source[here, :], 0.0)
            ref[here, :] = jnp.where(mine, roll(part, -half), other)
        ahead_c = jnp.concatenate([blank, ahead_c], 1)
        ahead_r = jnp.concatenate([blank, ahead_r], 1)
        beyond = jnp.where(at_end, ahead_r, 1.0)
        beyond = jnp.where(ghost, rho[here, :], beyond)
        dense = roll(parts[4], -half)
        speed = roll(parts[3], -half)
        rho[here, :] = jnp.where(mine, dense, beyond)
        hard = jnp.where(at_end, TIME_STEP * (ahead_r * ahead_c * ahead_c), 0.0)
        hard = jnp.where(ghost, stiff[here, :], hard)
        stiff[here, :] = jnp.where(mine, TIME_STEP * (dense * speed * speed), hard)

    def middle(r, k):
        here = pl.ds(r, k)
        place_rows(r + MARGIN, k, [ref[here, :] for ref in own], ahead[0][here, :], ahead[1][here, :])

    for_rows(0, height, middle)
    last = pl.ds(height - 1, 1)
    above, below = [], []
    for k in range(5):
        last_own = jnp.broadcast_to(own[k][last, :], (TILE, LANES))
        one, two = ghost_rows(up, down, k, last_own)
        above.append(one)
        below.append(two)
    at = pl.ds(5 * TILE, TILE)
    one, two = up[at, :], down[at, :]
    last_ahead = jnp.broadcast_to(ahead[1][last, :], (TILE, extra))
    one_r = jnp.where(depth == 0, 1.0, one[:, extra:])
    two_r = jnp.where(depth == lax.axis_size("depth") - 1, last_ahead, two[:, extra:])
    place_rows(TILE, TILE, above, one[:, :extra], one_r)
    place_rows(height + MARGIN, TILE, below, two[:, :extra], two_r)
    for e in (0, n - TILE):
        here = pl.ds(e, TILE)
        for ref in (p, u, w, stiff):
            ref[here, :] = jnp.zeros((TILE, LANES), jnp.float32)
        rho[here, :] = jnp.ones((TILE, LANES), jnp.float32)

    def coefs(r, k):
        here = pl.ds(r, k)
        dense = rho[here, :]
        ax[here, :] = (2.0 * TIME_STEP) / (dense + roll(dense, -1))
        az[here, :] = (2.0 * TIME_STEP) / (dense + rho[pl.ds(r + 1, k), :])
        al[here, :] = TIME_STEP / dense

    for_rows(0, n - TILE, coefs)
    at = pl.ds(TILE, TILE)
    az[at, :] = jnp.where(depth == 0, 0.0, az[at, :])
    base = depth * height

    def local_row(row):
        row = row - base
        inside = jnp.logical_and(row >= -TILE, row < height + TILE)
        return row + MARGIN, inside

    for t in range(ITERS):
        edge = jnp.where(at_end, half - 1 + offsets[t], FAR)
        taken = jnp.where(at_end, -1, half + t)

        def speeds(r, k):
            here = pl.ds(r, k)
            lanes = lane_ids(k)
            now = p[here, :]
            dead = lanes > edge
            slope = jnp.where(lanes == edge, al[here, :], ax[here, :])
            slope = jnp.where(dead, 0.0, slope)
            fast = u[here, :] - slope * (roll(now, -1) - now)
            u[here, :] = jnp.where(lanes == taken, gu[here, :], fast)
            slope = jnp.where(dead, 0.0, az[here, :])
            deep = w[here, :] - slope * (p[pl.ds(r + 1, k), :] - now)
            w[here, :] = jnp.where(lanes == taken, gw[here, :], deep)

        def press(r, k):
            here = pl.ds(r, k)
            lanes = lane_ids(k)
            fast = u[here, :]
            down_ = w[here, :] - w[pl.ds(r - 1, k), :]
            hard = jnp.where(lanes > edge, 0.0, stiff[here, :])
            found = p[here, :] - hard * ((fast - roll(fast, 1)) + down_)
            if t < ITERS - 1:
                found = jnp.where(lanes == taken + 1, jnp.where(at_end, found, gp[here, :]), found)
            p[here, :] = found

        for_rows(0, n - TILE, speeds)
        for_rows(TILE, n - TILE, press)
        reach = jnp.where(at_end, LANES - 1, half + t)
        inject(p, sources, wavelet, t, local_row, place * LANES + half, reach)

    n_done = n_first - 2 * MARGIN
    total = offsets[ITERS]

    def merge(shift, source, r, k):
        there = pl.ds(r, k)
        lanes = lane_ids(k)
        from_right = jnp.logical_or(lanes >= half + SKEW, lanes < SKEW)
        from_right = jnp.logical_or(from_right, jnp.logical_and(at_end, lanes < total))
        for f, ref in enumerate((p, u, w)):
            right = roll(ref[pl.ds(r + MARGIN, k), :], half)
            merged[f, there, :] = jnp.where(from_right, right, source[f, pl.ds(r - shift, k), :])

    for_rows(0, MARGIN, functools.partial(merge, 0, second_done))
    for_rows(MARGIN, MARGIN + n_done, functools.partial(merge, MARGIN, first_done))
    for_rows(MARGIN + n_done, height, functools.partial(merge, n_done, second_done))

    more = extra - SKEW - WIDTH
    start = SKEW + WIDTH

    def done_rows(r):
        if r < MARGIN:
            return second_done, 0
        if r < MARGIN + n_done:
            return first_done, MARGIN
        return second_done, n_done

    def join(fields):
        lanes = lane_ids(fields[0].shape[0])
        found = jnp.where(lanes < start + 2 * more, roll(fields[1], more), roll(fields[2], 2 * more))
        return jnp.where(lanes < start + more, fields[0], found)

    def beside(one, one_shift, two, two_shift, r, k):
        lanes = lane_ids(k)
        a = join([one[f, pl.ds(r - one_shift, k), :] for f in range(3)])
        b = join([two[f, pl.ds(r + height // 2 - two_shift, k), :] for f in range(3)])
        rest[pl.ds(r, k), :] = jnp.where(between(lanes, start, start + 3 * more), a, roll(b, LANES // 2))

    cuts = {0, height // 2, MARGIN, MARGIN + n_done, MARGIN - height // 2}
    cuts |= {MARGIN + n_done - height // 2}
    cuts = sorted(x for x in cuts if 0 <= x <= height // 2)
    for low, high in zip(cuts[:-1], cuts[1:]):
        one, one_shift = done_rows(low)
        two, two_shift = done_rows(low + height // 2)
        for_rows(low, high, functools.partial(beside, one, one_shift, two, two_shift))


def last_kernel(height, n_first, extra, shifts, merged, first, second, rest, *outs):
    place = lax.axis_index("range")
    at_end = place == lax.axis_size("range") - 1
    total = offsets_of(shifts)[ITERS]
    n_done = n_first - 2 * MARGIN
    more = extra - SKEW - WIDTH
    start = SKEW + WIDTH
    turn = LANES - total

    def build(source, shift, upper, r, k):
        here = pl.ds(r, k)
        lanes = lane_ids(k)
        near = source[pl.ds(r - shift, k), :]
        far = rest[here, :] if not upper else roll(rest[pl.ds(r - height // 2, k), :], LANES // 2)
        theirs = jnp.logical_and(between(lanes, SKEW, total), jnp.logical_not(at_end))
        for f, out in enumerate(outs):
            got = jnp.where(lanes < start, roll(near, -WIDTH * f), roll(far, -more * f))
            out[here, :] = pltpu.roll(jnp.where(theirs, got, merged[f, here, :]), turn, 1)

    cuts = sorted({0, MARGIN, height // 2, MARGIN + n_done, height})
    for low, high in zip(cuts[:-1], cuts[1:]):
        if low < MARGIN:
            source, shift = second, 0
        elif low < MARGIN + n_done:
            source, shift = first, MARGIN
        else:
            source, shift = second, n_done
        for_rows(low, high, functools.partial(build, source, shift, low >= height // 2))


def moved(x, axis, by):
    size = lax.axis_size(axis)
    return lax.ppermute(x, axis, [(i, i + by) for i in range(size) if 0 <= i + by < size])


def block(rows, at=0, lanes=LANES):
    return pl.BlockSpec((rows, lanes), lambda i: (at, 0))


def whole(x):
    return pl.BlockSpec(x.shape, lambda i: (0,) * len(x.shape))


def scalars(count):
    return [pl.BlockSpec(memory_space=pltpu.SMEM)] * count


def call(kernel, name, ins, specs, outs, scratch):
    return pl.pallas_call(
        kernel,
        name=name,
        grid=(1,),
        in_specs=specs,
        out_specs=[whole(x) for x in outs],
        out_shape=outs,
        scratch_shapes=scratch,
        compiler_params=pltpu.CompilerParams(vmem_limit_bytes=56 * 1024 * 1024),
    )(*ins)


def real(*shape):
    return jax.ShapeDtypeStruct(shape, jnp.float32)


def room(*shape):
    return pltpu.VMEM(shape, jnp.float32)


def shards(
    pressure,
    vel_range,
    vel_depth,
    sound_speed,
    density,
    ahead_speed,
    ahead_density,
    shifts,
    sources,
    wavelet,
):
    height, breadth = pressure.shape
    extra = ahead_speed.shape[1]
    assert breadth == LANES and SKEW + WIDTH < extra < LANES
    assert height % 512 == 0
    own = (pressure, vel_range, vel_depth, sound_speed, density)
    ahead = (ahead_speed, ahead_density)
    small = (shifts, sources, wavelet)

    split = height * 3 // 4
    n_first = split + 2 * MARGIN
    last = height // TILE - 1
    plane_a, done_a, slant_a, to_up, to_down = call(
        functools.partial(first_kernel, n_first, height),
        "first",
        (*small, *own, *own, *ahead, *ahead),
        [
            *scalars(3),
            *[block(n_first)] * 5,
            *[block(TILE, last)] * 5,
            *[block(TILE, 0, extra)] * 2,
            *[block(TILE, last, extra)] * 2,
        ],
        [
            real(split, LANES),
            real(3, split, LANES),
            real(split, LANES),
            real(6 * TILE, LANES),
            real(6 * TILE, LANES),
        ],
        [room(n_first, LANES)] * 3 + [room(ITERS, n_first, LANES)] * 3,
    )
    near = moved(plane_a, "range", -1)
    down = moved(to_up, "depth", -1)
    up = moved(to_down, "depth", 1)

    rest_rows = height - split
    n_second = 3 * MARGIN + rest_rows + MARGIN
    plane_b, done_b, slant = call(
        functools.partial(second_kernel, n_second, height, n_first),
        "second",
        (*small, *own, *own, up, down, slant_a),
        [
            *scalars(3),
            *[block(2 * MARGIN)] * 5,
            *[block(rest_rows, split // rest_rows)] * 5,
            whole(up),
            whole(down),
            whole(slant_a),
        ],
        [
            real(rest_rows, LANES),
            real(3, rest_rows, LANES),
            real((height + 2 * MARGIN) // GROUPS, LANES),
        ],
        [room(n_second, LANES)] * 3
        + [room(ITERS, n_second, LANES)] * 3
        + [room(n_second, LANES)] * 5
        + [room(height + 2 * MARGIN, LANES)],
    )
    slant = moved(slant, "range", -1)
    edge = moved(plane_b, "range", -1)

    merged, rest = call(
        functools.partial(right_kernel, height, n_first, extra),
        "right",
        (*small, *own, *ahead, up, down, slant, done_a, done_b),
        [*scalars(3), *[whole(x) for x in (*own, *ahead, up, down, slant, done_a, done_b)]],
        [real(3, height, LANES), real(height // 2, LANES)],
        [room(height + 2 * MARGIN, LANES)] * 12,
    )
    rest = lax.cond(
        jnp.sum(shifts) > SKEW + WIDTH,
        lambda x: moved(x, "range", -1),
        jnp.zeros_like,
        rest,
    )
    return tuple(
        call(
            functools.partial(last_kernel, height, n_first, extra),
            "last",
            (shifts, merged, near, edge, rest),
            [*scalars(1), *[whole(x) for x in (merged, near, edge, rest)]],
            [real(height, LANES)] * 3,
            [],
        )
    )


def solution(mesh):
    field = P("depth", "range")
    strip = P("depth", None)
    return jax.shard_map(
        shards,
        mesh=mesh,
        in_specs=(field,) * 5 + (strip,) * 2 + (P(),) * 3,
        out_specs=(field,) * 3,
        check_vma=False,
    )
```

time: 142 us -> 80.8 us (0.57)
  Pallas kernels: 0 us -> 49.3 us
  starting transfers between devices: 57.5 us -> 10.3 us
  other arithmetic: 21.3 us -> 0.7 us
  waiting for transfers between devices: 22.9 us -> 8.29 us
  local copies, waits for them, and re-layouts: 22.9 us -> 9.31 us
  matrix products: 10.8 us -> 0 us
  between operations: 5.17 us -> 1.36 us
    pallas_call x0 -> x4, Pallas kernels: none -> 49.3 us  [call(): pl.pallas_call(kernel, name=name, grid=(1,), in_specs=specs, out_specs=[w...]
    ppermute x21 -> x5, starting transfers between devices: 57.5 us -> 10.3 us  [moved(): lax.ppermute(x, axis, [(i, i + by) for i in range(size) if 0 <= i + by <...]
    ppermute x21 -> x5, waiting for transfers between devices: 22.9 us -> 8.29 us  [moved(): lax.ppermute(x, axis, [(i, i + by) for i in range(size) if 0 <= i + by <...]
    select_n x9 -> x0, other arithmetic: 14.3 us -> none  [the longest x4 9.74 us: shards(): vel_depth = jnp.where(live[None, :], fresh, vel_depth)]
    dot_general x4 -> x0, matrix products: 10.8 us -> none  [shards(): jnp.dot((depth_onehot * amplitude[:, None]).T, range_onehot, precision=la...]
    slice x30 -> x0, local copies, waits for them, and re-layouts: 9.49 us -> none  [the longest x4 2.12 us: shards(): upper_edge = upper_rims(vel_depth[-1:])]
    unnamed x58 -> x16, local copies, waits for them, and re-layouts: 12.8 us -> 8.59 us
    ppermute x2 -> x0, other arithmetic: 2.49 us -> none  [shifted(): return lax.ppermute(shard, axis, pairs)]
  transfers between devices with their start and end apart: 21 -> 5, of which waited for: 8 -> 2; matrix products, arithmetic and copies ran while one was open for 22% -> 2% of each run, Pallas kernels for 0% -> 37%
where the time goes in v1:
time: 80.8 us; the launch traced here: 79.2 us
  Pallas kernels  49.3 us (61%)
  starting transfers between devices  10.3 us (13%)
  local copies, waits for them, and re-layouts  9.31 us (12%)
  waiting for transfers between devices  8.29 us (10%)
  between operations  1.36 us (2%)
    pallas_call x4, Pallas kernels, call(): pl.pallas_call(kernel, name=name, grid=(1,), in_specs=specs, out_specs=[w...  49.3 us
    ppermute x5, starting transfers between devices, moved(): lax.ppermute(x, axis, [(i, i + by) for i in range(size) if 0 <= i + by <...  10.3 us
    unnamed x16, local copies, waits for them, and re-layouts  8.59 us
    ppermute x5, waiting for transfers between devices, moved(): lax.ppermute(x, axis, [(i, i + by) for i in range(size) if 0 <= i + by <...  8.29 us
  transfers between devices with their start and end apart: 5, of which 2 were waited for; matrix products, arithmetic and copies ran while one was open for 2% of the time, Pallas kernels for 37%

profile of v1, /device:TPU:1, one launch (start us, length us, event | category | flops | bytes accessed | tf_op | source)
XLA Modules:
  0.0 79.2 jit_solution(15597036088202087354)
XLA Ops:
  0.6 1.3 %copy.21.refs_1_ = s32[8,2]{1,0:T(8,128)} copy(s32[8,2]{0,1:T(2,128)} %param.20) | data formatting | bytes 128 | tf_op args[8]
  2.0 1.3 %copy.22.refs_2_ = f32[8,4]{1,0:T(8,128)} copy(f32[8,4]{0,1:T(4,128)} %param.21) | data formatting | bytes 256 | tf_op args[9]
  3.3 1.9 %copy.23.refs_13_.refs_15_.refs_8_ = f32[1024,64]{1,0:T(8,128)} copy(f32[1024,64]{0,1:T(8,128)} %param.17) | data formatting | bytes 524288 | tf_op args[5]
  5.3 1.9 %copy.24.refs_14_.refs_16_.refs_9_ = f32[1024,64]{1,0:T(8,128)} copy(f32[1024,64]{0,1:T(8,128)} %param.18) | data formatting | bytes 524288 | tf_op args[6]
  7.2 13.8 %first.1 = (f32[768,128]{1,0:T(8,128)}, f32[3,768,128]{2,1,0:T(8,128)}, f32[768,128]{1,0:T(8,128)}, f32[48,128]{1,0:T(8,128)}, f32[48,128]{1,0:T(8,128)}) custom-call(s32[4]{0:T(128)} %shifts.1, s32[8,2]{1,0:T(8,128)} %copy.21.refs_1_, f32[8,4]{1,0:T(8,128)} %copy.22.refs_2_, f32[1024,128]{1,0:T(8,128)} %refs_3_.5, f32[1024,128]{1,0:T(8,128)} %refs_4_.5, ...), custom_call_target="tpu_custom_call" | custom-call | tf_op jit(solution)/shard_map/first/pallas_call | solution.py:470
  21.0 1.3 %collective-permute-start.4 = (f32[768,128]{1,0:T(8,128)}, f32[768,128]{1,0:T(8,128)S(1)}, u32[]{:S(2)}, u32[]{:S(2)}) collective-permute-start(f32[768,128]{1,0:T(8,128)} %get-tuple-element.24), channel_id=1, source_target_pairs={{4,0},{8,4},{12,8},{16,12},{20,16},{24,20},{28,24},{5,1},{9,5},{13... | collective-permute-start | bytes 1179656 | tf_op jit(solution)/shard_map/ppermute | solution.py:454
  22.3 4.5 %collective-permute-start.1 = (f32[48,128]{1,0:T(8,128)}, f32[48,128]{1,0:T(8,128)S(1)}, u32[]{:S(2)}, u32[]{:S(2)}) collective-permute-start(f32[48,128]{1,0:T(8,128)} %get-tuple-element.17), channel_id=1, source_target_pairs={{0,1},{1,2},{2,3},{4,5},{5,6},{6,7},{8,9},{9,10},{10,11},{12,13},{... | collective-permute-start | bytes 73736 | tf_op jit(solution)/shard_map/ppermute | solution.py:454
  26.8 1.9 %collective-permute-start.2 = (f32[48,128]{1,0:T(8,128)}, f32[48,128]{1,0:T(8,128)S(1)}, u32[]{:S(2)}, u32[]{:S(2)}) collective-permute-start(f32[48,128]{1,0:T(8,128)} %get-tuple-element.18), channel_id=1, source_target_pairs={{1,0},{2,1},{3,2},{5,4},{6,5},{7,6},{9,8},{10,9},{11,10},{13,12},{... | collective-permute-start | bytes 73736 | tf_op jit(solution)/shard_map/ppermute | solution.py:454
  28.8 0.0 collective-permute-done.1.refs_13_.refs_10_
  28.8 0.0 copy-start.2
  28.8 3.7 %collective-permute-done.2.refs_14_.refs_11_ = f32[48,128]{1,0:T(8,128)S(1)} collective-permute-done((f32[48,128]{1,0:T(8,128)}, f32[48,128]{1,0:T(8,128)S(1)}, u32[]{:S(2)}, u32[]{:S(2)}) %collective-permute-start.2) | collective-permute-done | bytes 24608 | tf_op jit(solution)/shard_map/ppermute | solution.py:454
  32.5 0.0 copy-start.3
  32.5 0.0 copy-done.2
  32.5 0.6 copy-done.3
  33.1 0.0 copy-start.5
  33.1 7.1 %second.1 = (f32[256,128]{1,0:T(8,128)}, f32[3,256,128]{2,1,0:T(8,128)}, f32[176,128]{1,0:T(8,128)}) custom-call(s32[4]{0:T(128)} %shifts.1, s32[8,2]{1,0:T(8,128)} %copy.21.refs_1_, f32[8,4]{1,0:T(8,128)} %copy.22.refs_2_, f32[1024,128]{1,0:T(8,128)} %refs_3_.5, f32[1024,128]{1,0:T(8,128)} %refs_4_.5, f32[1024,128]{1,0:T(8,128)} %refs_5_.5, ...), custom_call_target="tpu_custom_call" | custom-call | tf_op jit(solution)/shard_map/second/pallas_call | solution.py:470
  40.2 1.3 %collective-permute-start.5 = (f32[256,128]{1,0:T(8,128)}, f32[256,128]{1,0:T(8,128)S(1)}, u32[]{:S(2)}, u32[]{:S(2)}) collective-permute-start(f32[256,128]{1,0:T(8,128)} %get-tuple-element.25), channel_id=1, source_target_pairs={{4,0},{8,4},{12,8},{16,12},{20,16},{24,20},{28,24},{5,1},{9,5},{13... | collective-permute-start | bytes 393224 | tf_op jit(solution)/shard_map/ppermute | solution.py:454
  41.5 1.3 %collective-permute-start.3 = (f32[176,128]{1,0:T(8,128)}, f32[176,128]{1,0:T(8,128)S(1)}, u32[]{:S(2)}, u32[]{:S(2)}) collective-permute-start(f32[176,128]{1,0:T(8,128)} %get-tuple-element.20), channel_id=1, source_target_pairs={{4,0},{8,4},{12,8},{16,12},{20,16},{24,20},{28,24},{5,1},{9,5},{13... | collective-permute-start | bytes 270344 | tf_op jit(solution)/shard_map/ppermute | solution.py:454
  42.8 0.0 copy-done.5
  42.8 0.7 reduce_sum.9
  44.1 4.6 %collective-permute-done.3.refs_12_ = f32[176,128]{1,0:T(8,128)S(1)} collective-permute-done((f32[176,128]{1,0:T(8,128)}, f32[176,128]{1,0:T(8,128)S(1)}, u32[]{:S(2)}, u32[]{:S(2)}) %collective-permute-start.3) | collective-permute-done | bytes 90144 | tf_op jit(solution)/shard_map/ppermute | solution.py:454
  48.7 0.0 copy-start.4
  48.7 0.6 copy-done.4
  49.3 22.5 %right.1 = (f32[3,1024,128]{2,1,0:T(8,128)}, f32[512,128]{1,0:T(8,128)S(1)}) custom-call(s32[4]{0:T(128)} %shifts.1, s32[8,2]{1,0:T(8,128)} %copy.21.refs_1_, f32[8,4]{1,0:T(8,128)} %copy.22.refs_2_, f32[1024,128]{1,0:T(8,128)} %refs_3_.5, f32[1024,128]{1,0:T(8,128)} %refs_4_.5, f32[1024,128]{1,0:T(8,128)} %refs_5_.5, f32[1024,128]{1,0:T(8,128)} %refs_6_.5, ...), custom_call_target="tpu_custom_call" | custom-call | tf_op jit(solution)/shard_map/right/pallas_call | solution.py:470
  71.8 0.7 conditional.1
  71.8 0.7 broadcast.2
  72.5 0.0 collective-permute-done.5.second
  72.5 0.0 collective-permute-done.4.first
  72.5 0.0 copy-start
  72.5 0.6 copy-done.1
  73.2 0.1 copy-done
  73.3 5.9 %last.1 = (f32[1024,128]{1,0:T(8,128)}, f32[1024,128]{1,0:T(8,128)}, f32[1024,128]{1,0:T(8,128)}) custom-call(s32[4]{0:T(128)} %shifts.1, f32[3,1024,128]{2,1,0:T(8,128)} %get-tuple-element.23.merged, f32[768,128]{1,0:T(8,128)} %copy-done, f32[256,128]{1,0:T(8,128)} %copy-done.1, f32[512,128]{1,0:T(8,128)} %get-tuple-element.27.rest), custom_call_target="tpu_custom_call" | custom-call | tf_op jit(solution)/shard_map/last/pallas_call | solution.py:470
  (1 shorter events, 0.0 us)
Async XLA Ops:
  21.0 51.5 %collective-permute-start.4 = (f32[768,128]{1,0:T(8,128)}, f32[768,128]{1,0:T(8,128)S(1)}, u32[]{:S(2)}, u32[]{:S(2)}) collective-permute-start(f32[768,128]{1,0:T(8,128)} %get-tuple-element.24), channel_id=1, source_target_pairs={{4,0},{8,4},{12,8},{16,12},{20,16},{24,20},{28,24},{5,1},{9,5},{13... | collective-permute-start | bytes 1179656 | tf_op jit(solution)/shard_map/ppermute | solution.py:454
  22.3 6.4 %collective-permute-start.1 = (f32[48,128]{1,0:T(8,128)}, f32[48,128]{1,0:T(8,128)S(1)}, u32[]{:S(2)}, u32[]{:S(2)}) collective-permute-start(f32[48,128]{1,0:T(8,128)} %get-tuple-element.17), channel_id=1, source_target_pairs={{0,1},{1,2},{2,3},{4,5},{5,6},{6,7},{8,9},{9,10},{10,11},{12,13},{... | collective-permute-start | bytes 73736 | tf_op jit(solution)/shard_map/ppermute | solution.py:454
  26.8 5.7 %collective-permute-start.2 = (f32[48,128]{1,0:T(8,128)}, f32[48,128]{1,0:T(8,128)S(1)}, u32[]{:S(2)}, u32[]{:S(2)}) collective-permute-start(f32[48,128]{1,0:T(8,128)} %get-tuple-element.18), channel_id=1, source_target_pairs={{1,0},{2,1},{3,2},{5,4},{6,5},{7,6},{9,8},{10,9},{11,10},{13,12},{... | collective-permute-start | bytes 73736 | tf_op jit(solution)/shard_map/ppermute | solution.py:454
  28.8 3.7 %copy-start.2 = (f32[48,128]{1,0:T(8,128)}, f32[48,128]{1,0:T(8,128)S(1)}, u32[]{:S(2)}) copy-start(f32[48,128]{1,0:T(8,128)S(1)} %collective-permute-done.1.refs_13_.refs_10_) | copy-start | bytes 73732
  32.5 0.6 copy-start.3
  33.1 9.7 %copy-start.5 = (s32[4]{0:T(128)S(1)}, s32[4]{0:T(128)}, u32[]{:S(2)}) copy-start(s32[4]{0:T(128)} %shifts.1) | copy-start | bytes 52
  40.2 32.3 %collective-permute-start.5 = (f32[256,128]{1,0:T(8,128)}, f32[256,128]{1,0:T(8,128)S(1)}, u32[]{:S(2)}, u32[]{:S(2)}) collective-permute-start(f32[256,128]{1,0:T(8,128)} %get-tuple-element.25), channel_id=1, source_target_pairs={{4,0},{8,4},{12,8},{16,12},{20,16},{24,20},{28,24},{5,1},{9,5},{13... | collective-permute-start | bytes 393224 | tf_op jit(solution)/shard_map/ppermute | solution.py:454
  41.5 7.2 %collective-permute-start.3 = (f32[176,128]{1,0:T(8,128)}, f32[176,128]{1,0:T(8,128)S(1)}, u32[]{:S(2)}, u32[]{:S(2)}) collective-permute-start(f32[176,128]{1,0:T(8,128)} %get-tuple-element.20), channel_id=1, source_target_pairs={{4,0},{8,4},{12,8},{16,12},{20,16},{24,20},{28,24},{5,1},{9,5},{13... | collective-permute-start | bytes 270344 | tf_op jit(solution)/shard_map/ppermute | solution.py:454
  48.7 0.6 copy-start.4
  72.5 0.6 copy-start.1
  72.5 0.8 copy-start
